TPU v7x, 32 devices: a whole 2x2x4 slice. The times are simulated.
32 devices in a mesh: dp: 8 (over z, y), mp: 4 (over x, core).
Axes of the slice: x: 2, y: 2, z: 4, core: 2. Of those that a mesh axis runs over, the one named last changes fastest.
Arguments:
- tokens: bfloat16 [6144, 768], P(('dp', 'mp')), may hold values from -6 to 6
- obs_mask: int32 [96, 64], P(('dp', 'mp')), may hold values 0 or 1
- norm_gains: float32 [5, 768], replicated, may hold values from 0.1 to 1.9
- attn_in: bfloat16 [2, 3, 768, 768], P(None, None, 'dp', 'mp'), may hold values from -0.21875 to 0.21875
- attn_out: bfloat16 [2, 768, 768], P(None, 'mp', 'dp'), may hold values from -0.21875 to 0.21875
- mlp_in: bfloat16 [2, 768, 3072], P(None, 'dp', 'mp'), may hold values from -0.21875 to 0.21875
- mlp_out: bfloat16 [2, 3072, 768], P(None, 'mp', 'dp'), may hold values from -0.109375 to 0.109375
- embodiment: int32 [96, 1], P('dp'), may hold values from 0 to 24; in each aligned block of 12 rows (0 to 11, 12 to 23, ...) no two rows name the same one
- levels: int32 [96, 2], P('dp'), may hold values from 0 to 19
- actions: bfloat16 [96, 2, 56], P('dp'), may hold values from -1 to 1
- noise: bfloat16 [96, 2, 56], P('dp'), may hold values from -5 to 5
- action_dims: int32 [25], replicated, may hold values from 7 to 14
- head_read: bfloat16 [32, 768, 256], P('dp'), may hold values from -0.21875 to 0.21875
- head_act: bfloat16 [32, 56, 256], P('dp'), may hold values from -0.75 to 0.75
- time_table: bfloat16 [32, 20, 256], P('dp'), may hold values from -5 to 5
- block_in: bfloat16 [32, 256, 256], P('dp'), may hold values from -0.375 to 0.375
- block_out: bfloat16 [32, 256, 256], P('dp'), may hold values from -0.375 to 0.375
- head_out: bfloat16 [32, 256, 56], P('dp'), may hold values from -0.375 to 0.375
Outputs:
- readout_grad: bfloat16 [96, 2, 768], P(('dp', 'mp'))
- grad_read: float32 [32, 768, 256], P('dp', 'mp')
- grad_act: float32 [32, 56, 256], P('dp')
- grad_time: float32 [32, 20, 256], P('dp')
- grad_block_in: float32 [32, 256, 256], P('dp')
- grad_block_out: float32 [32, 256, 256], P('dp')
- grad_head_out: float32 [32, 256, 56], P('dp')
Inputs may be any that keep to these rules, and one draw needn't show every extreme that they name: Within each aligned block of 12 samples (those of one dp index) no embodiment appears twice; every embodiment appears in some block.
All inputs are finite; a program needn't handle non-finite values. No bound on the sum of `obs_mask` on one device may be relied on, other than what follows from the above.
Results may differ from a plain program's by a relative error of at most 0.024.
Values may be sent and summed in bfloat16 or wider, within the bound.
A program may use at most 64 MiB of HBM per device.

v0:
```python
import math

import jax
import jax.numpy as jnp
from jax import lax
from jax.sharding import PartitionSpec as P

D = 768
HDIM = 64
EMB = 25
READ = 2
LEVELS = 20
ADIM_MAX = 14
ACT = 56


norm_eps = 1e-05


def normalize(values, scale_gain):
    center = values - jnp.mean(values, axis=-1, keepdims=True)
    spread = jnp.mean(center * center, axis=-1, keepdims=True)
    return center * lax.rsqrt(spread + norm_eps) * scale_gain


def allowed_keys(observed):
    length = observed.shape[1]
    position = jnp.arange(length)
    visible = (observed == 1) & (position < length - READ)[None, :]
    itself = position[:, None] == position[None, :]
    return visible[:, None, :] | itself[None, :, :]


def attend(queries, key_rows, value_rows, allowed):
    scores = jnp.einsum(
        "sqhd,skhd->shqk", queries, key_rows, preferred_element_type=jnp.float32
    ) * HDIM ** (-0.5)
    weights = jnp.where(allowed[:, None, :, :], jnp.exp(scores), 0.0)
    shares = (weights / jnp.sum(weights, axis=-1, keepdims=True)).astype(jnp.bfloat16)
    context = jnp.einsum("shqk,skhd->sqhd", shares, value_rows, preferred_element_type=jnp.float32)
    return context.astype(jnp.bfloat16)


def plan():
    steps_up = (jnp.arange(LEVELS, dtype=jnp.float32) + 1.0) / LEVELS
    anchor = math.cos(0.008 / 1.008 * math.pi / 2) ** 2
    return jnp.cos((steps_up + 0.008) / 1.008 * (math.pi / 2)) ** 2 / anchor


def noisy_pair(level_ids, clean, noise_draw, table):
    picked = (level_ids[..., None] == jnp.arange(LEVELS)).astype(jnp.float32)
    kept = jnp.sum(picked * table, axis=-1)[..., None]
    mixed = jnp.sqrt(kept) * clean.astype(jnp.float32) + jnp.sqrt(1.0 - kept) * noise_draw.astype(
        jnp.float32
    )
    return mixed.astype(jnp.bfloat16)


def tail(first, target, weight_mask, inner_weight, outer_weight, final_weight):
    highest = lax.Precision.HIGHEST
    active = jax.nn.silu(first).astype(jnp.bfloat16)
    inner = jnp.dot(active, inner_weight, preferred_element_type=jnp.float32, precision=highest)
    second = jax.nn.silu(inner).astype(jnp.bfloat16)
    hidden = first + jnp.dot(
        second, outer_weight, preferred_element_type=jnp.float32, precision=highest
    )
    third = jax.nn.silu(hidden).astype(jnp.bfloat16)
    predicted = jnp.dot(third, final_weight, preferred_element_type=jnp.float32, precision=highest)
    differ = predicted - target
    return 0.5 * jnp.sum(weight_mask * differ * differ)


def gather_rows(normed, observed):
    return (
        lax.all_gather(normed, "mp", axis=0, tiled=True),
        lax.all_gather(observed, "mp", axis=0, tiled=True),
    )


def reduce_rows(partial_value):
    return lax.psum_scatter(
        partial_value.astype(jnp.bfloat16), "mp", scatter_dimension=0, tiled=True
    ).astype(jnp.float32)


def head_grads(first, inner_weight, outer_weight, final_weight, target, weight_mask):

    def head_loss(first_in, inner_in, outer_in, final_in):
        return tail(first_in, target, weight_mask, inner_in, outer_in, final_in)

    loss_value, pullback = jax.vjp(head_loss, first, inner_weight, outer_weight, final_weight)
    return pullback(jnp.ones((), jnp.float32))


def on_device(
    tokens,
    obs_mask,
    norm_gains,
    attn_in,
    attn_out,
    mlp_in,
    mlp_out,
    embodiment,
    levels,
    actions,
    noise,
    action_dims,
    head_read,
    head_act,
    time_table,
    block_in,
    block_out,
    head_out,
):
    group_width = attn_in.shape[3]
    heads_local = group_width // HDIM
    samples_local = obs_mask.shape[0]
    length = obs_mask.shape[1]
    layer_count = attn_in.shape[0]
    residual = tokens.astype(jnp.float32)
    for layer_index in range(layer_count):
        normed = normalize(residual, norm_gains[2 * layer_index]).astype(jnp.bfloat16)
        gathered, mask_group = gather_rows(normed, obs_mask)
        samples_group = mask_group.shape[0]
        columns = gathered
        projected = jnp.einsum(
            "td,jdc->jtc",
            columns,
            lax.all_gather(attn_in[layer_index], "dp", axis=1, tiled=True),
            preferred_element_type=jnp.float32,
        )
        projected = projected.astype(jnp.bfloat16).reshape(
            3, samples_group, length, heads_local, HDIM
        )
        context = attend(
            projected[0], projected[1], projected[2], allowed_keys(mask_group)
        ).reshape(-1, group_width)
        partial_value = jnp.dot(
            context,
            lax.all_gather(attn_out[layer_index], "dp", axis=1, tiled=True),
            preferred_element_type=jnp.float32,
        )
        residual = residual + reduce_rows(partial_value)
        normed = normalize(residual, norm_gains[2 * layer_index + 1]).astype(jnp.bfloat16)
        gathered, mask_group = gather_rows(normed, obs_mask)
        raised = jnp.dot(
            gathered,
            lax.all_gather(mlp_in[layer_index], "dp", axis=0, tiled=True),
            preferred_element_type=jnp.float32,
        )
        hidden = jax.nn.gelu(raised, approximate=True).astype(jnp.bfloat16)
        partial_value = jnp.dot(
            hidden,
            lax.all_gather(mlp_out[layer_index], "dp", axis=1, tiled=True),
            preferred_element_type=jnp.float32,
        )
        residual = residual + reduce_rows(partial_value)
    ending = residual.reshape(samples_local, length, D)[:, length - READ :, :]
    readouts = normalize(ending, norm_gains[2 * layer_count]).astype(jnp.bfloat16)
    table = plan()
    heads_dev = head_read.shape[0]
    peers = lax.axis_size("dp")
    slot_count = heads_dev * peers
    my_model = lax.axis_index("mp")
    my_owner = lax.axis_index("dp")
    features = lax.all_to_all(readouts, "mp", split_axis=2, concat_axis=0, tiled=True)
    owners = embodiment[:, 0]
    feature_width = features.shape[2]
    paired = jnp.concatenate([noisy_pair(levels, actions, noise, table), noise], axis=-1)
    send_features = (
        jnp.zeros((slot_count, READ, feature_width), jnp.bfloat16).at[owners].set(features)
    )
    send_paired = jnp.zeros((slot_count, READ, 2 * ACT), jnp.bfloat16).at[owners].set(paired)
    send_levels = jnp.full((slot_count, READ), -1, jnp.int32).at[owners].set(levels)
    got_features, got_paired, got_levels = (
        lax.all_to_all(
            send_features.reshape(peers, heads_dev * READ, feature_width),
            "dp",
            split_axis=0,
            concat_axis=0,
            tiled=True,
        ),
        lax.all_to_all(
            send_paired.reshape(peers, heads_dev * READ, 2 * ACT),
            "dp",
            split_axis=0,
            concat_axis=0,
            tiled=True,
        ),
        lax.all_to_all(
            send_levels.reshape(peers, heads_dev * READ),
            "dp",
            split_axis=0,
            concat_axis=0,
            tiled=True,
        ),
    )

    def by_head(values):
        trailing = values.shape[2:]
        values = values.reshape((peers, heads_dev, READ) + trailing)
        values = jnp.moveaxis(values, 1, 0)
        return values.reshape((heads_dev, peers * READ) + trailing)

    head_features = by_head(got_features)
    head_paired = by_head(got_paired)
    head_levels = by_head(got_levels)
    head_noisy = head_paired[..., :ACT]
    head_target = head_paired[..., ACT:].astype(jnp.float32)
    head_onehot = (head_levels[..., None] == jnp.arange(LEVELS)).astype(jnp.bfloat16)
    slot_ids = my_owner * heads_dev + jnp.arange(heads_dev)
    dims_here = jnp.sum(
        jnp.where(jnp.arange(EMB)[None, :] == slot_ids[:, None], action_dims[None, :], 0), axis=1
    )
    column = jnp.arange(ACT) % ADIM_MAX
    weight_mask = (head_levels >= 0).astype(jnp.float32)[..., None] * (
        column[None, None, :] < dims_here[:, None, None]
    ).astype(jnp.float32)
    others = jnp.einsum("hna,hac->hnc", head_noisy, head_act, preferred_element_type=jnp.float32)
    others = others + jnp.einsum(
        "hnl,hlc->hnc", head_onehot, time_table, preferred_element_type=jnp.float32
    )
    read_weight = lax.dynamic_slice_in_dim(head_read, my_model * feature_width, feature_width, 1)
    first = (
        lax.psum(
            jnp.einsum(
                "hnd,hdc->hnc", head_features, read_weight, preferred_element_type=jnp.float32
            ).astype(jnp.bfloat16),
            "mp",
        ).astype(jnp.float32)
        + others
    )
    grad_first, grad_inner, grad_outer, grad_final = jax.vmap(head_grads)(
        first,
        block_in.astype(jnp.float32),
        block_out.astype(jnp.float32),
        head_out.astype(jnp.float32),
        head_target,
        weight_mask,
    )
    grad_bf = grad_first.astype(jnp.bfloat16)
    grad_readin = jnp.einsum(
        "hnd,hnc->hdc", head_features, grad_bf, preferred_element_type=jnp.float32
    )
    grad_actin = jnp.einsum("hna,hnc->hac", head_noisy, grad_bf, preferred_element_type=jnp.float32)
    grad_timein = jnp.einsum(
        "hnl,hnc->hlc", head_onehot, grad_bf, preferred_element_type=jnp.float32
    )
    backward = jnp.einsum(
        "hnc,hdc->hnd", grad_bf, read_weight, preferred_element_type=jnp.float32
    ).astype(jnp.bfloat16)
    backward = jnp.moveaxis(backward.reshape(heads_dev, peers, READ, feature_width), 0, 1).reshape(
        peers, heads_dev * READ, feature_width
    )
    arrived = lax.all_to_all(backward, "dp", split_axis=0, concat_axis=0, tiled=True)
    arrived = arrived.reshape(slot_count, READ, feature_width)[owners]
    arrived = lax.all_to_all(arrived, "mp", split_axis=0, concat_axis=2, tiled=True)
    return (arrived, grad_readin, grad_actin, grad_timein, grad_inner, grad_outer, grad_final)


def solution(mesh):
    placed = (
        P(("dp", "mp"), None),
        P(("dp", "mp"), None),
        P(),
        P(None, None, "dp", "mp"),
        P(None, "mp", "dp"),
        P(None, "dp", "mp"),
        P(None, "mp", "dp"),
        P("dp", None),
        P("dp", None),
        P("dp", None, None),
        P("dp", None, None),
        P(),
        P("dp", None, None),
        P("dp", None, None),
        P("dp", None, None),
        P("dp", None, None),
        P("dp", None, None),
        P("dp", None, None),
    )
    return jax.shard_map(
        on_device,
        mesh=mesh,
        in_specs=placed,
        out_specs=(
            P(("dp", "mp"), None, None),
            P("dp", "mp", None),
            P("dp", None, None),
            P("dp", None, None),
            P("dp", None, None),
            P("dp", None, None),
            P("dp", None, None),
        ),
        check_vma=False,
    )
```

profile of v0, /device:TPU:0, one launch (start us, length us, event | category | flops | bytes accessed | tf_op | source)
XLA Modules:
  0.0 542.9 jit_solution(12618972121489949078)
XLA Ops:
  11.4 1.9 fusion.54
  14.1 38.8 %all-gather = bf16[1,3,768,192]{3,1,0,2:T(4,128)(2,1)S(1)} all-gather(bf16[1,3,96,192]{3,1,0,2:T(4,128)(2,1)S(1)} %copy.243), channel_id=2, replica_groups=mesh['dp'=8,'mp'=4] {'dp'}, dimensions={2}, use_global_device_ids=true | all-gather | bytes 995328 | tf_op jit(solution)/shard_map/all_gather | solution.py:129
  52.9 2.0 copy.209
  54.9 5.2 all-gather.8
  61.5 32.1 %all-gather.1 = bf16[1,192,768]{1,0,2:T(2,128)(2,1)S(1)} all-gather(bf16[1,192,96]{1,0,2:T(2,128)(2,1)S(1)} %copy.244), channel_id=3, replica_groups=mesh['dp'=8,'mp'=4] {'dp'}, dimensions={2}, use_global_device_ids=true | all-gather | bytes 331776 | tf_op jit(solution)/shard_map/all_gather | solution.py:140
  95.6 2.2 fusion.118
  98.4 1.3 squeeze.46
  99.8 1.3 squeeze.44
  101.1 2.7 fusion.19
  103.8 2.1 fusion.20
  106.8 1.6 convolution_convert_fusion.3
  110.1 23.1 %reduce-scatter.5.cloned.1.call-done = bf16[192,768]{1,0:T(8,128)(2,1)} async-done(((bf16[768,768]{1,0:T(8,128)(2,1)}), bf16[192,768]{1,0:T(8,128)(2,1)}) %reduce-scatter.5.cloned.1.call-update) | async-done | bytes 294928 | tf_op jit(solution)/shard_map/reduce_scatter | solution.py:81
  136.5 15.6 %all-gather.26.cloned.1.call-done = bf16[1,768,768]{2,1,0:T(8,128)(2,1)} async-done(((bf16[1,96,768]{2,1,0:T(8,128)(2,1)}), bf16[1,768,768]{2,1,0:T(8,128)(2,1)}) %all-gather.26.cloned.1.call-update) | async-done | bytes 1179664 | tf_op jit(solution)/shard_map/all_gather | solution.py:148
  152.1 42.4 %all-gather.28.cloned.1.call-done = bf16[1,768,768]{1,2,0:T(8,128)(2,1)} async-done(((bf16[1,768,96]{1,2,0:T(8,128)(2,1)}), bf16[1,768,768]{1,2,0:T(8,128)(2,1)}) %all-gather.28.cloned.1.call-update) | async-done | bytes 1179664 | tf_op jit(solution)/shard_map/all_gather | solution.py:154
  194.5 17.7 %all-gather.20.cloned.1.call-done = bf16[768,768]{1,0:T(8,128)(2,1)} async-done(((bf16[192,768]{1,0:T(8,128)(2,1)}), bf16[768,768]{1,0:T(8,128)(2,1)}) %all-gather.20.cloned.1.call-update) | async-done | bytes 1179664 | tf_op jit(solution)/shard_map/all_gather | solution.py:75
  212.2 5.2 convolution_convert_fusion.2
  217.5 25.7 %reduce-scatter.7.cloned.1.call-done = bf16[192,768]{1,0:T(8,128)(2,1)} async-done(((bf16[768,768]{1,0:T(8,128)(2,1)}), bf16[192,768]{1,0:T(8,128)(2,1)}) %reduce-scatter.7.cloned.1.call-update) | async-done | bytes 294928 | tf_op jit(solution)/shard_map/reduce_scatter | solution.py:81
  245.7 38.6 %all-gather.4 = bf16[1,3,768,192]{3,1,0,2:T(4,128)(2,1)} all-gather(bf16[1,3,96,192]{3,1,0,2:T(4,128)(2,1)S(1)} %copy.245), channel_id=6, replica_groups=mesh['dp'=8,'mp'=4] {'dp'}, dimensions={2}, use_global_device_ids=true | all-gather | bytes 995328 | tf_op jit(solution)/shard_map/all_gather | solution.py:129
  284.3 3.4 copy.218
  287.8 32.2 %all-gather.5 = bf16[1,192,768]{1,0,2:T(2,128)(2,1)S(1)} all-gather(bf16[1,192,96]{1,0,2:T(2,128)(2,1)S(1)} %copy.246), channel_id=7, replica_groups=mesh['dp'=8,'mp'=4] {'dp'}, dimensions={2}, use_global_device_ids=true | all-gather | bytes 331776 | tf_op jit(solution)/shard_map/all_gather | solution.py:140
  320.6 2.4 fusion.119
  323.1 1.3 squeeze.52
  326.3 2.8 fusion.17
  329.1 2.9 fusion.21
  332.1 1.5 copy.223
  334.0 1.6 convolution_convert_fusion.1
  337.1 22.9 %reduce-scatter.9.cloned.1.call-done = bf16[192,768]{1,0:T(8,128)(2,1)} async-done(((bf16[768,768]{1,0:T(8,128)(2,1)}), bf16[192,768]{1,0:T(8,128)(2,1)}) %reduce-scatter.9.cloned.1.call-update) | async-done | bytes 294928 | tf_op jit(solution)/shard_map/reduce_scatter | solution.py:81
  363.3 15.3 %all-gather.30.cloned.1.call-done = bf16[1,768,768]{2,1,0:T(8,128)(2,1)} async-done(((bf16[1,96,768]{2,1,0:T(8,128)(2,1)}), bf16[1,768,768]{2,1,0:T(8,128)(2,1)}) %all-gather.30.cloned.1.call-update) | async-done | bytes 1179664 | tf_op jit(solution)/shard_map/all_gather | solution.py:148
  378.6 42.6 %all-gather.32.cloned.1.call-done = bf16[1,768,768]{1,2,0:T(8,128)(2,1)} async-done(((bf16[1,768,96]{1,2,0:T(8,128)(2,1)}), bf16[1,768,768]{1,2,0:T(8,128)(2,1)}) %all-gather.32.cloned.1.call-update) | async-done | bytes 1179664 | tf_op jit(solution)/shard_map/all_gather | solution.py:154
  421.2 17.7 %all-gather.24.cloned.1.call-done = bf16[768,768]{1,0:T(8,128)(2,1)} async-done(((bf16[192,768]{1,0:T(8,128)(2,1)}), bf16[768,768]{1,0:T(8,128)(2,1)}) %all-gather.24.cloned.1.call-update) | async-done | bytes 1179664 | tf_op jit(solution)/shard_map/all_gather | solution.py:75
  438.8 5.2 convolution_convert_fusion
  446.1 5.5 %all-to-all-start = ((s32[8,1,8]{2,1,0:T(1,128)}), s32[8,1,8]{2,1,0:T(1,128)S(1)}, u32[]{:S(2)}, u32[]{:S(2)}) async-start(s32[8,1,8]{2,1,0:T(1,128)} %bitcast.1), calls=%async_computation | async-start | bytes 8192 | tf_op jit(solution)/shard_map/all_to_all | solution.py:190
  453.0 2.0 scatter_fusion.1
  455.0 3.0 all-to-all-done
  458.0 3.3 all-to-all-start.3
  461.6 8.3 %reduce-scatter.11.cloned.1.call-done = bf16[192,768]{1,0:T(8,128)(2,1)} async-done(((bf16[768,768]{1,0:T(8,128)(2,1)}), bf16[192,768]{1,0:T(8,128)(2,1)}) %reduce-scatter.11.cloned.1.call-update) | async-done | bytes 294928 | tf_op jit(solution)/shard_map/reduce_scatter | solution.py:81
  472.4 2.2 fusion.117
  475.8 3.6 all-to-all-start.1
  479.6 3.4 all-to-all-done.1
  485.8 5.5 %all-to-all-start.2 = ((bf16[8,8,192]{2,1,0:T(8,128)(2,1)}), bf16[8,8,192]{2,1,0:T(8,128)(2,1)S(1)}, u32[]{:S(2)}, u32[]{:S(2)}) async-start(bf16[8,8,192]{2,1,0:T(8,128)(2,1)} %reshape.234), calls=%async_computation.6 | async-start | bytes 65536 | tf_op jit(solution)/shard_map/all_to_all | solution.py:176
  491.5 6.5 %all-to-all-done.2 = bf16[8,8,192]{2,1,0:T(8,128)(2,1)S(1)} async-done(((bf16[8,8,192]{2,1,0:T(8,128)(2,1)}), bf16[8,8,192]{2,1,0:T(8,128)(2,1)S(1)}, u32[]{:S(2)}, u32[]{:S(2)}) %all-to-all-start.2) | async-done | bytes 24608 | tf_op jit(solution)/shard_map/all_to_all | solution.py:176
  498.3 10.3 %psum.7 = bf16[4,16,256]{2,1,0:T(8,128)(2,1)S(1)} all-reduce(bf16[4,16,256]{2,1,0:T(8,128)(2,1)S(1)} %convolution_convert_fusion.10), channel_id=1, replica_groups=mesh['dp'=8,'mp'=4] {'mp'}, use_global_device_ids=true, to_apply=%region_19.20 | all-reduce | flops 16384 | bytes 65536 | tf_op jit(solution)/shard_map/psum | solution.py:225
  510.5 1.6 fusion.107
  512.6 1.6 fusion.105
  516.8 3.3 all-to-all-start.4
  521.1 5.7 %all-to-all-done.4 = bf16[8,8,192]{2,1,0:T(8,128)(2,1)S(1)} async-done(((bf16[8,8,192]{2,1,0:T(8,128)(2,1)}), bf16[8,8,192]{2,1,0:T(8,128)(2,1)S(1)}, u32[]{:S(2)}, u32[]{:S(2)}) %all-to-all-start.4) | async-done | bytes 24608 | tf_op jit(solution)/shard_map/all_to_all | solution.py:255
  528.0 3.2 all-to-all-start.5
  532.2 2.9 all-to-all-done.5
  (182 shorter events, 43.7 us)
Async XLA Ops:
  8.0 490.1 %copy-start = (bf16[4,768,256]{2,1,0:T(8,128)(2,1)S(1)}, bf16[4,768,256]{2,1,0:T(8,128)(2,1)}, u32[]{:S(2)}) copy-start(bf16[4,768,256]{2,1,0:T(8,128)(2,1)} %param.30) | copy-start | bytes 4718596
  8.0 5.3 copy-start.9
  8.0 87.6 %all-gather.18.cloned.1.call-start = ((), (), s32[]{:S(2)}) async-start(), calls=%async_computation.10 | async-start | bytes 1474560 | tf_op jit(solution)/shard_map/all_gather | solution.py:75
  13.3 119.9 %reduce-scatter.5.cloned.1.call-start = ((), (), s32[]{:S(2)}) async-start(), calls=%async_computation.11 | async-start | bytes 1474560 | tf_op jit(solution)/shard_map/reduce_scatter | solution.py:81
  52.9 2.0 copy-start.19
  52.9 7.8 %copy-start.14 = (bf16[2,192,96]{2,1,0:T(8,128)(2,1)S(1)}, bf16[2,192,96]{2,1,0:T(8,128)(2,1)}, u32[]{:S(2)}) copy-start(bf16[2,192,96]{2,1,0:T(8,128)(2,1)} %param.22) | copy-start | bytes 221188
  60.7 34.9 %copy-start.6 = (bf16[1,3,768,192]{2,3,1,0:T(8,128)(2,1)S(1)}, bf16[1,3,768,192]{2,3,1,0:T(8,128)(2,1)}, u32[]{:S(2)}) copy-start(bf16[1,3,768,192]{2,3,1,0:T(8,128)(2,1)} %copy.209) | copy-start | bytes 2654212
  98.4 2.7 copy-start.15
  101.1 2.7 copy-start.7
  106.7 1.6 copy-start.10
  108.3 1.0 copy-start.11
  108.3 24.9 %copy-start.1 = (bf16[192,768]{1,0:T(8,128)(2,1)S(1)}, bf16[192,768]{1,0:T(8,128)(2,1)}, u32[]{:S(2)}) copy-start(bf16[192,768]{1,0:T(8,128)(2,1)} %param.18) | copy-start | bytes 884740
  108.3 43.8 %all-gather.26.cloned.1.call-start = ((), (), s32[]{:S(2)}) async-start(), calls=%async_computation.18 | async-start | bytes 1327104 | tf_op jit(solution)/shard_map/all_gather | solution.py:148
  109.2 85.4 %all-gather.28.cloned.1.call-start = ((), (), s32[]{:S(2)}) async-start(), calls=%async_computation.19 | async-start | bytes 1327104 | tf_op jit(solution)/shard_map/all_gather | solution.py:154
  110.0 102.2 %all-gather.20.cloned.1.call-start = ((), (), s32[]{:S(2)}) async-start(), calls=%async_computation.12 | async-start | bytes 1474560 | tf_op jit(solution)/shard_map/all_gather | solution.py:75
  133.2 2.4 copy-start.2
  136.5 106.7 %reduce-scatter.7.cloned.1.call-start = ((), (), s32[]{:S(2)}) async-start(), calls=%async_computation.13 | async-start | bytes 1474560 | tf_op jit(solution)/shard_map/reduce_scatter | solution.py:81
  217.5 103.1 %all-gather.22.cloned.1.call-start = ((), (), s32[]{:S(2)}) async-start(), calls=%async_computation.14 | async-start | bytes 1474560 | tf_op jit(solution)/shard_map/all_gather | solution.py:75
  244.4 1.2 copy-start.8
  245.5 114.5 %reduce-scatter.9.cloned.1.call-start = ((), (), s32[]{:S(2)}) async-start(), calls=%async_computation.15 | async-start | bytes 1474560 | tf_op jit(solution)/shard_map/reduce_scatter | solution.py:81
  284.3 3.4 copy-start.12
  335.6 43.0 %all-gather.30.cloned.1.call-start = ((), (), s32[]{:S(2)}) async-start(), calls=%async_computation.20 | async-start | bytes 1327104 | tf_op jit(solution)/shard_map/all_gather | solution.py:148
  336.3 84.9 %all-gather.32.cloned.1.call-start = ((), (), s32[]{:S(2)}) async-start(), calls=%async_computation.21 | async-start | bytes 1327104 | tf_op jit(solution)/shard_map/all_gather | solution.py:154
  337.0 101.8 %all-gather.24.cloned.1.call-start = ((), (), s32[]{:S(2)}) async-start(), calls=%async_computation.16 | async-start | bytes 1474560 | tf_op jit(solution)/shard_map/all_gather | solution.py:75
  360.0 2.4 copy-start.3
  363.2 106.6 %reduce-scatter.11.cloned.1.call-start = ((), (), s32[]{:S(2)}) async-start(), calls=%async_computation.17 | async-start | bytes 1474560 | tf_op jit(solution)/shard_map/reduce_scatter | solution.py:81
  444.0 0.7 copy-start.20
  444.0 0.8 copy-start.22
  444.0 7.9 %copy-start.17 = (bf16[12,2,56]{2,1,0:T(2,128)(2,1)S(1)}, bf16[12,2,56]{2,1,0:T(2,128)(2,1)}, u32[]{:S(2)}) copy-start(bf16[12,2,56]{2,1,0:T(2,128)(2,1)} %param.28) | copy-start | bytes 8068
  444.0 7.9 %copy-start.18 = (bf16[12,2,56]{2,1,0:T(2,128)(2,1)S(1)}, bf16[12,2,56]{2,1,0:T(2,128)(2,1)}, u32[]{:S(2)}) copy-start(bf16[12,2,56]{2,1,0:T(2,128)(2,1)} %param.27) | copy-start | bytes 8068
  444.0 8.0 %copy-start.23 = (s32[25]{0:T(128)S(1)}, s32[25]{0:T(128)}, u32[]{:S(2)}) copy-start(s32[25]{0:T(128)} %param.29) | copy-start | bytes 304
  446.1 11.9 %all-to-all-start = ((s32[8,1,8]{2,1,0:T(1,128)}), s32[8,1,8]{2,1,0:T(1,128)S(1)}, u32[]{:S(2)}, u32[]{:S(2)}) async-start(s32[8,1,8]{2,1,0:T(1,128)} %bitcast.1), calls=%async_computation | async-start | bytes 8192 | tf_op jit(solution)/shard_map/all_to_all | solution.py:190
  458.0 17.7 %all-to-all-start.3 = ((bf16[8,8,112]{2,1,0:T(8,128)(2,1)}), bf16[8,8,112]{2,1,0:T(8,128)(2,1)S(1)}, u32[]{:S(2)}, u32[]{:S(2)}) async-start(bf16[8,8,112]{2,1,0:T(8,128)(2,1)} %bitcast.30), calls=%async_computation.7 | async-start | bytes 32768 | tf_op jit(solution)/shard_map/all_to_all | solution.py:183
  472.4 18.9 %copy-start.13 = (bf16[4,56,256]{2,1,0:T(8,128)(2,1)S(1)}, bf16[4,56,256]{2,1,0:T(8,128)(2,1)}, u32[]{:S(2)}) copy-start(bf16[4,56,256]{2,1,0:T(8,128)(2,1)} %param.31) | copy-start | bytes 344068
  474.6 33.9 %copy-start.16 = (bf16[4,20,256]{2,0,1:T(4,128)(2,1)S(1)}, bf16[4,20,256]{2,0,1:T(4,128)(2,1)}, u32[]{:S(2)}) copy-start(bf16[4,20,256]{2,0,1:T(4,128)(2,1)} %param.32) | copy-start | bytes 122884
  475.8 33.0 %copy-start.4 = (bf16[4,256,256]{2,1,0:T(8,128)(2,1)S(1)}, bf16[4,256,256]{2,1,0:T(8,128)(2,1)}, u32[]{:S(2)}) copy-start(bf16[4,256,256]{2,1,0:T(8,128)(2,1)} %param.33) | copy-start | bytes 1572868
  475.8 7.2 %all-to-all-start.1 = ((bf16[4,2,576]{2,1,0:T(2,128)(2,1)}), bf16[4,2,576]{2,1,0:T(2,128)(2,1)S(1)}, u32[]{:S(2)}, u32[]{:S(2)}) async-start(bf16[4,2,576]{2,1,0:T(2,128)(2,1)} %reshape.298), calls=%async_computation.5 | async-start | bytes 20480 | tf_op jit(solution)/shard_map/all_to_all | solution.py:166
  483.7 25.3 %copy-start.5 = (bf16[4,256,256]{2,1,0:T(8,128)(2,1)S(1)}, bf16[4,256,256]{2,1,0:T(8,128)(2,1)}, u32[]{:S(2)}) copy-start(bf16[4,256,256]{2,1,0:T(8,128)(2,1)} %param.34) | copy-start | bytes 1572868
  485.8 12.2 %all-to-all-start.2 = ((bf16[8,8,192]{2,1,0:T(8,128)(2,1)}), bf16[8,8,192]{2,1,0:T(8,128)(2,1)S(1)}, u32[]{:S(2)}, u32[]{:S(2)}) async-start(bf16[8,8,192]{2,1,0:T(8,128)(2,1)} %reshape.234), calls=%async_computation.6 | async-start | bytes 65536 | tf_op jit(solution)/shard_map/all_to_all | solution.py:176
  491.5 17.7 %copy-start.21 = (bf16[4,256,56]{1,2,0:T(8,128)(2,1)S(1)}, bf16[4,256,56]{1,2,0:T(8,128)(2,1)}, u32[]{:S(2)}) copy-start(bf16[4,256,56]{1,2,0:T(8,128)(2,1)} %param.35) | copy-start | bytes 344068
  516.8 10.0 %all-to-all-start.4 = ((bf16[8,8,192]{2,1,0:T(8,128)(2,1)}), bf16[8,8,192]{2,1,0:T(8,128)(2,1)S(1)}, u32[]{:S(2)}, u32[]{:S(2)}) async-start(bf16[8,8,192]{2,1,0:T(8,128)(2,1)} %copy.237), calls=%async_computation.8 | async-start | bytes 65536 | tf_op jit(solution)/shard_map/all_to_all | solution.py:255
  528.0 7.1 %all-to-all-start.5 = ((bf16[12,2,192]{2,1,0:T(2,128)(2,1)}), bf16[12,2,192]{2,1,0:T(2,128)(2,1)S(1)}, u32[]{:S(2)}, u32[]{:S(2)}) async-start(bf16[12,2,192]{2,1,0:T(2,128)(2,1)} %gather_fusion), calls=%async_computation.9 | async-start | bytes 24576 | tf_op jit(solution)/shard_map/all_to_all | solution.py:257
Sparse Core Ops, SparseCore 0:
  13.4 20.1 all-gather.17
  108.5 24.7 reduce-scatter.4
  217.6 25.6 reduce-scatter.6
  335.7 24.2 reduce-scatter.8
  444.2 25.6 reduce-scatter.10
Sparse Core Ops, SparseCore 1:
  111.6 40.5 all-gather.25
  154.8 39.7 all-gather.27
  196.5 15.6 all-gather.19
  245.6 17.3 all-gather.21
  338.5 40.0 all-gather.29
  381.4 39.7 all-gather.31
  423.2 15.6 all-gather.23
where the time goes:
time: 544 us; the launch traced here: 543 us
  waiting for transfers between devices  254 us (47%)
  blocking collectives  157 us (29%)
  matrix products  37.6 us (7%)
  local copies, waits for them, and re-layouts  33.4 us (6%)
  starting transfers between devices  25.1 us (5%)
  other arithmetic  19.4 us (4%)
  between operations  15.9 us (3%)
    all_gather x2, waiting for transfers between devices, on_device(): lax.all_gather(mlp_out[layer_index], 'dp', axis=1, tiled=True)  85 us
    reduce_scatter x4, waiting for transfers between devices, reduce_rows(): lax.psum_scatter(partial_value.astype(jnp.bfloat16), 'mp', scatter_dimens...  80 us
    all_gather x2, blocking collectives, on_device(): lax.all_gather(attn_in[layer_index], 'dp', axis=1, tiled=True)  77.4 us
    all_gather x2, blocking collectives, on_device(): lax.all_gather(attn_out[layer_index], 'dp', axis=1, tiled=True)  64.3 us
    all_gather x4, waiting for transfers between devices, gather_rows(): lax.all_gather(normed, 'mp', axis=0, tiled=True)  35.4 us
    all_gather x2, waiting for transfers between devices, on_device(): lax.all_gather(mlp_in[layer_index], 'dp', axis=0, tiled=True)  30.9 us
  transfers between devices with their start and end apart: 18, of which 15 were waited for; matrix products, arithmetic and copies ran while one was open for 6% of the time, Pallas kernels for 0%

commit v1 on v0

v1 whole, which is shorter than its diff:
```python
import functools
import math

import jax
import jax.numpy as jnp
from jax import lax
from jax.experimental import pallas as pl
from jax.experimental.pallas import tpu as pltpu
from jax.sharding import PartitionSpec as P

HDIM = 64
EMB = 25
READ = 2
LEVELS = 20
ADIM_MAX = 14

norm_eps = 1e-05
MESH_ID = pl.DeviceIdType.MESH


def normalize(values, scale_gain):
    center = values - jnp.mean(values, axis=-1, keepdims=True)
    spread = jnp.mean(center * center, axis=-1, keepdims=True)
    return center * lax.rsqrt(spread + norm_eps) * scale_gain


def plan():
    steps_up = (jnp.arange(LEVELS, dtype=jnp.float32) + 1.0) / LEVELS
    anchor = math.cos(0.008 / 1.008 * math.pi / 2) ** 2
    return jnp.cos((steps_up + 0.008) / 1.008 * (math.pi / 2)) ** 2 / anchor


def noisy_pair(level_ids, clean, noise_draw, table):
    picked = (level_ids[..., None] == jnp.arange(LEVELS)).astype(jnp.float32)
    kept = jnp.sum(picked * table, axis=-1)[..., None]
    mixed = jnp.sqrt(kept) * clean.astype(jnp.float32) + jnp.sqrt(1.0 - kept) * noise_draw.astype(
        jnp.float32
    )
    return mixed.astype(jnp.bfloat16)


def ring_place(index, size):
    if size % 2:
        return index
    odd = index % 2
    return (1 - odd) * (index // 2) + odd * (size - 1 - index // 2)


def ring_index(place, size):
    if size % 2:
        return place
    back = place // (size // 2)
    return (1 - back) * (2 * place) + back * (2 * (size - 1 - place) + 1)


def ring_parts(rows, tile=16):
    if rows % (2 * tile):
        return [(0, rows)], []
    half = rows // 2
    return [[(way * half + start, tile) for start in range(0, half, tile)] for way in range(2)]


def exchange_kernel(n_dp, n_mp, kinds, *refs):
    count = len(kinds)
    ins, outs = refs[:count], refs[count : 2 * count]
    sems = refs[2 * count :]
    local_sem = sems[-1]
    my_dp, my_mp = lax.axis_index("dp"), lax.axis_index("mp")
    place = ring_place(my_dp, n_dp)

    talk_mp = any(kind in ("split", "cast") for kind in kinds)
    talk_dp = "swap" in kinds
    talk_ring = "ring" in kinds
    barrier = pltpu.get_barrier_semaphore()
    greeted = 0
    if talk_mp:
        for offset in range(1, n_mp):
            pl.semaphore_signal(
                barrier, inc=1, device_id={"mp": (my_mp + offset) % n_mp}, device_id_type=MESH_ID
            )
            greeted += 1
    if talk_dp:
        for offset in range(1, n_dp):
            pl.semaphore_signal(
                barrier, inc=1, device_id={"dp": (my_dp + offset) % n_dp}, device_id_type=MESH_ID
            )
            greeted += 1
    elif talk_ring:
        for way in (1, n_dp - 1):
            pl.semaphore_signal(
                barrier,
                inc=1,
                device_id={"dp": ring_index((place + way) % n_dp, n_dp)},
                device_id_type=MESH_ID,
            )
            greeted += 1
    pl.semaphore_wait(barrier, greeted)

    def ring_copies(item, step):
        source, landing = ins[item], outs[item]
        made = []
        for way, parts in enumerate(ring_parts(source.shape[0])):
            for chunk, (start, extent) in enumerate(parts):
                origin = ring_index((place + (n_dp - step if way == 0 else step)) % n_dp, n_dp)
                target = ring_index((place + (1 if way == 0 else n_dp - 1)) % n_dp, n_dp)
                rows = pl.ds(start, extent)
                spot = landing.at[origin, rows]
                made.append(
                    pltpu.make_async_remote_copy(
                        src_ref=source.at[rows] if step == 0 else spot,
                        dst_ref=spot,
                        send_sem=sems[2 * item].at[step, chunk, way],
                        recv_sem=sems[2 * item + 1].at[step, chunk, way],
                        device_id={"dp": target},
                        device_id_type=MESH_ID,
                    )
                )
        return made

    rings = [item for item in range(count) if kinds[item] == "ring"]
    flights = {item: ring_copies(item, 0) for item in rings}
    for item in rings:
        for copy in flights[item]:
            copy.start()
    direct = []
    keeps = []
    for item, kind in enumerate(kinds):
        source, landing = ins[item], outs[item]
        if kind == "ring":
            keeps.append(pltpu.make_async_copy(source, landing.at[my_dp], local_sem.at[item]))
            continue
        size, mine, axis = (n_dp, my_dp, "dp") if kind == "swap" else (n_mp, my_mp, "mp")
        for offset in range(1, size):
            peer = (mine + offset) % size
            copy = pltpu.make_async_remote_copy(
                src_ref=source if kind == "cast" else source.at[peer],
                dst_ref=landing.at[mine],
                send_sem=sems[2 * item].at[offset],
                recv_sem=sems[2 * item + 1].at[offset],
                device_id={axis: peer},
                device_id_type=MESH_ID,
            )
            copy.start()
            direct.append(copy)
        keeps.append(
            pltpu.make_async_copy(
                source if kind == "cast" else source.at[mine], landing.at[mine], local_sem.at[item]
            )
        )
    for keep in keeps:
        keep.start()
    sent = [copy for item in rings for copy in flights[item]]
    for step in range(1, n_dp - 1):
        for item in rings:
            following = ring_copies(item, step)
            for before, after in zip(flights[item], following):
                before.wait_recv()
                after.start()
            flights[item] = following
            sent = sent + following
    for item in rings:
        for copy in flights[item]:
            copy.wait_recv()
    for copy in direct:
        copy.wait_recv()
    for copy in sent + direct:
        copy.wait_send()
    for keep in keeps:
        keep.wait()


def exchange(ident, *pairs):
    n_dp, n_mp = lax.axis_size("dp"), lax.axis_size("mp")
    kinds = tuple(kind for kind, _ in pairs)
    arrays = [array for _, array in pairs]
    shapes, scratch = [], []
    for kind, array in pairs:
        lead = {"ring": (n_dp,), "cast": (n_mp,), "split": (), "swap": ()}[kind]
        shapes.append(jax.ShapeDtypeStruct(lead + array.shape, array.dtype))
        if kind == "ring":
            slots = (n_dp - 1, len(ring_parts(array.shape[0])[0]), 2)
        else:
            slots = (n_dp if kind == "swap" else n_mp,)
        scratch += [pltpu.SemaphoreType.DMA(slots), pltpu.SemaphoreType.DMA(slots)]
    scratch.append(pltpu.SemaphoreType.DMA((len(pairs),)))
    return pl.pallas_call(
        functools.partial(exchange_kernel, n_dp, n_mp, kinds),
        out_shape=shapes,
        in_specs=[pl.BlockSpec(memory_space=pltpu.VMEM)] * len(pairs),
        out_specs=[pl.BlockSpec(memory_space=pltpu.VMEM)] * len(pairs),
        scratch_shapes=scratch,
        compiler_params=pltpu.CompilerParams(collective_id=ident, has_side_effects=True),
        name="exchange%d" % ident,
    )(*arrays)


def attend(queries, key_rows, value_rows, allowed):
    scores = jnp.einsum(
        "sqhd,skhd->shqk", queries, key_rows, preferred_element_type=jnp.float32
    ) * HDIM ** (-0.5)
    weights = jnp.where(allowed[:, None, :, :], jnp.exp(scores), 0.0)
    shares = (weights / jnp.sum(weights, axis=-1, keepdims=True)).astype(jnp.bfloat16)
    context = jnp.einsum("shqk,skhd->sqhd", shares, value_rows, preferred_element_type=jnp.float32)
    return context.astype(jnp.bfloat16)


def dot32(left, right):
    return jnp.dot(left, right, preferred_element_type=jnp.float32)


def dot_turned(left, right):
    return lax.dot_general(
        left, right, (((1,), (1,)), ((), ())), preferred_element_type=jnp.float32
    )


def added(blocks):
    return jnp.sum(blocks.astype(jnp.float32), axis=0)


def tail(first, target, weight_mask, inner_weight, outer_weight, final_weight):
    highest = lax.Precision.HIGHEST
    active = jax.nn.silu(first).astype(jnp.bfloat16)
    inner = jnp.dot(active, inner_weight, preferred_element_type=jnp.float32, precision=highest)
    second = jax.nn.silu(inner).astype(jnp.bfloat16)
    hidden = first + jnp.dot(
        second, outer_weight, preferred_element_type=jnp.float32, precision=highest
    )
    third = jax.nn.silu(hidden).astype(jnp.bfloat16)
    predicted = jnp.dot(third, final_weight, preferred_element_type=jnp.float32, precision=highest)
    differ = predicted - target
    return 0.5 * jnp.sum(weight_mask * differ * differ)


def head_grads(first, inner_weight, outer_weight, final_weight, target, weight_mask):

    def head_loss(first_in, inner_in, outer_in, final_in):
        return tail(first_in, target, weight_mask, inner_in, outer_in, final_in)

    loss_value, pullback = jax.vjp(head_loss, first, inner_weight, outer_weight, final_weight)
    return pullback(jnp.ones((), jnp.float32))


def on_device(
    tokens,
    obs_mask,
    norm_gains,
    attn_in,
    attn_out,
    mlp_in,
    mlp_out,
    embodiment,
    levels,
    actions,
    noise,
    action_dims,
    head_read,
    head_act,
    time_table,
    block_in,
    block_out,
    head_out,
):
    model = tokens.shape[1]
    act = actions.shape[2]
    width = attn_in.shape[3]
    heads_local = width // HDIM
    samples_local, length = obs_mask.shape
    layer_count = attn_in.shape[0]
    n_mp, n_dp = lax.axis_size("mp"), lax.axis_size("dp")
    my_model, my_owner = lax.axis_index("mp"), lax.axis_index("dp")
    samples_group = samples_local * n_mp
    ident = iter(range(100))

    joined = [
        jnp.concatenate(
            [attn_in[layer, 0], attn_in[layer, 1], attn_in[layer, 2], attn_out[layer].T], axis=1
        )
        for layer in range(layer_count)
    ]
    lowered = [mlp_out[layer].T for layer in range(layer_count)]

    heads_dev = head_read.shape[0]
    slot_count = heads_dev * n_dp
    owners = embodiment[:, 0]
    table = plan()
    onto = (jnp.arange(slot_count)[:, None] == owners[None, :]).astype(jnp.bfloat16)
    spread_rows = jnp.einsum("es,rq->ersq", onto, jnp.eye(READ, dtype=jnp.bfloat16)).reshape(
        slot_count * READ, samples_group * READ
    )
    small = jnp.concatenate(
        [
            noisy_pair(levels, actions, noise, table),
            noise,
            (levels + 1)[..., None].astype(jnp.bfloat16),
        ],
        axis=-1,
    ).reshape(samples_group * READ, 2 * act + 1)
    small = jnp.pad(small, ((0, 0), (0, -small.shape[1] % 128)))
    small = dot32(spread_rows, small).astype(jnp.bfloat16)
    small = small.reshape(n_dp, heads_dev * READ, small.shape[1])

    residual = tokens.astype(jnp.float32)
    wide = None
    allowed = None
    mask_group = None
    got_small = None
    position = jnp.arange(length)
    for layer in range(layer_count):
        final = layer == layer_count - 1
        normed = normalize(residual, norm_gains[2 * layer]).astype(jnp.bfloat16)
        if layer == 0:
            sends = [("cast", normed), ("cast", obs_mask), ("swap", small), ("ring", joined[0])]
        else:
            sends = [("cast", normed)]
        if final:
            ends = residual.reshape(samples_local, length, model)[:, length - READ :, :]
            sends += [("cast", ends), ("ring", mlp_in[layer]), ("ring", lowered[layer])]
        got = list(exchange(next(ident), *sends))
        gathered = got.pop(0).reshape(-1, model)
        if layer == 0:
            mask_group = got.pop(0).reshape(samples_group, length)
            got_small = got.pop(0)
            wide = got.pop(0).reshape(model, -1)
            visible = (mask_group == 1) & (position < length - READ)[None, :]
            itself = position[:, None] == position[None, :]
            allowed = visible[:, None, :] | itself[None, :, :]
        if final:
            ends = got.pop(0).reshape(samples_group * READ, model)
            upper = got.pop(0).reshape(model, -1)
            lower = got.pop(0).reshape(model, -1)
            asking = gathered.reshape(samples_group, length, model)[:, length - READ :, :]
            queries = dot32(asking.reshape(-1, model), wide[:, :width]).astype(jnp.bfloat16)
            queries = queries.reshape(samples_group, READ, heads_local, HDIM)
            both = dot32(gathered, wide[:, width : 3 * width]).astype(jnp.bfloat16)
            keys_at = both[:, :width].reshape(samples_group, length, heads_local, HDIM)
            values_at = both[:, width:].reshape(samples_group, length, heads_local, HDIM)
            context = attend(queries, keys_at, values_at, allowed[:, length - READ :, :])
            partial_value = dot_turned(context.reshape(-1, width), wide[:, 3 * width :])
            (terms,) = exchange(next(ident), ("cast", partial_value.astype(jnp.bfloat16)))
            ends = ends + added(terms)
            normed = normalize(ends, norm_gains[2 * layer + 1]).astype(jnp.bfloat16)
            hidden = jax.nn.gelu(dot32(normed, upper), approximate=True).astype(jnp.bfloat16)
            partial_value = dot_turned(hidden, lower)
            (terms,) = exchange(next(ident), ("cast", partial_value.astype(jnp.bfloat16)))
            ends = ends + added(terms)
            break
        projected = dot32(gathered, wide[:, : 3 * width]).astype(jnp.bfloat16)
        split = [
            projected[:, part * width : (part + 1) * width].reshape(
                samples_group, length, heads_local, HDIM
            )
            for part in range(3)
        ]
        context = attend(split[0], split[1], split[2], allowed).reshape(-1, width)
        partial_value = dot_turned(context, wide[:, 3 * width :]).astype(jnp.bfloat16)
        terms, upper = exchange(
            next(ident),
            ("split", partial_value.reshape(n_mp, -1, model)),
            ("ring", mlp_in[layer]),
        )
        residual = residual + added(terms)
        normed = normalize(residual, norm_gains[2 * layer + 1]).astype(jnp.bfloat16)
        gathered, lower = exchange(next(ident), ("cast", normed), ("ring", lowered[layer]))
        raised = dot32(gathered.reshape(-1, model), upper.reshape(model, -1))
        hidden = jax.nn.gelu(raised, approximate=True).astype(jnp.bfloat16)
        partial_value = dot_turned(hidden, lower.reshape(model, -1)).astype(jnp.bfloat16)
        terms, wide = exchange(
            next(ident),
            ("split", partial_value.reshape(n_mp, -1, model)),
            ("ring", joined[layer + 1]),
        )
        wide = wide.reshape(model, -1)
        residual = residual + added(terms)

    readouts = normalize(ends, norm_gains[2 * layer_count]).astype(jnp.bfloat16)
    send = dot32(spread_rows, readouts).astype(jnp.bfloat16)
    (got_features,) = exchange(
        next(ident), ("swap", send.reshape(n_dp, heads_dev * READ, model))
    )

    def by_head(values):
        values = values.reshape(n_dp, heads_dev, READ, values.shape[-1])
        return jnp.moveaxis(values, 1, 0).reshape(heads_dev, n_dp * READ, values.shape[-1])

    head_features = by_head(got_features)
    head_small = by_head(got_small)
    head_noisy = head_small[..., :act]
    head_target = head_small[..., act : 2 * act].astype(jnp.float32)
    head_levels = head_small[..., 2 * act].astype(jnp.int32) - 1
    head_onehot = (head_levels[..., None] == jnp.arange(LEVELS)).astype(jnp.bfloat16)
    slot_ids = my_owner * heads_dev + jnp.arange(heads_dev)
    dims_here = jnp.sum(
        jnp.where(jnp.arange(EMB)[None, :] == slot_ids[:, None], action_dims[None, :], 0), axis=1
    )
    column = jnp.arange(act) % ADIM_MAX
    weight_mask = (head_levels >= 0).astype(jnp.float32)[..., None] * (
        column[None, None, :] < dims_here[:, None, None]
    ).astype(jnp.float32)
    others = jnp.einsum("hna,hac->hnc", head_noisy, head_act, preferred_element_type=jnp.float32)
    others = others + jnp.einsum(
        "hnl,hlc->hnc", head_onehot, time_table, preferred_element_type=jnp.float32
    )
    first = (
        jnp.einsum("hnd,hdc->hnc", head_features, head_read, preferred_element_type=jnp.float32)
        + others
    )
    grad_first, grad_inner, grad_outer, grad_final = jax.vmap(head_grads)(
        first,
        block_in.astype(jnp.float32),
        block_out.astype(jnp.float32),
        head_out.astype(jnp.float32),
        head_target,
        weight_mask,
    )
    grad_bf = grad_first.astype(jnp.bfloat16)
    backward = jnp.einsum(
        "hnc,hdc->hnd", grad_bf, head_read, preferred_element_type=jnp.float32
    ).astype(jnp.bfloat16)
    backward = jnp.moveaxis(backward.reshape(heads_dev, n_dp, READ, model), 0, 1)
    (arrived,) = exchange(
        next(ident), ("swap", backward.reshape(n_dp, heads_dev * READ, model))
    )
    mine = lax.dynamic_slice_in_dim(
        spread_rows, my_model * (samples_local * READ), samples_local * READ, 1
    )
    returned = lax.dot_general(
        mine,
        arrived.reshape(slot_count * READ, model),
        (((0,), (0,)), ((), ())),
        preferred_element_type=jnp.float32,
    ).astype(jnp.bfloat16)
    feature_width = model // n_mp
    own_features = lax.dynamic_slice_in_dim(
        head_features, my_model * feature_width, feature_width, 2
    )
    grad_readin = jnp.einsum(
        "hnd,hnc->hdc", own_features, grad_bf, preferred_element_type=jnp.float32
    )
    grad_actin = jnp.einsum("hna,hnc->hac", head_noisy, grad_bf, preferred_element_type=jnp.float32)
    grad_timein = jnp.einsum(
        "hnl,hnc->hlc", head_onehot, grad_bf, preferred_element_type=jnp.float32
    )
    return (
        returned.reshape(samples_local, READ, model),
        grad_readin,
        grad_actin,
        grad_timein,
        grad_inner,
        grad_outer,
        grad_final,
    )


def solution(mesh):
    placed = (
        P(("dp", "mp"), None),
        P(("dp", "mp"), None),
        P(),
        P(None, None, "dp", "mp"),
        P(None, "mp", "dp"),
        P(None, "dp", "mp"),
        P(None, "mp", "dp"),
        P("dp", None),
        P("dp", None),
        P("dp", None, None),
        P("dp", None, None),
        P(),
        P("dp", None, None),
        P("dp", None, None),
        P("dp", None, None),
        P("dp", None, None),
        P("dp", None, None),
        P("dp", None, None),
    )
    return jax.shard_map(
        on_device,
        mesh=mesh,
        in_specs=placed,
        out_specs=(
            P(("dp", "mp"), None, None),
            P("dp", "mp", None),
            P("dp", None, None),
            P("dp", None, None),
            P("dp", None, None),
            P("dp", None, None),
            P("dp", None, None),
        ),
        check_vma=False,
    )
```

time: 544 us -> 250 us (0.46)
  waiting for transfers between devices: 254 us -> 0 us
  Pallas kernels: 0 us -> 171 us
  blocking collectives: 157 us -> 0 us
  starting transfers between devices: 25.1 us -> 0 us
  between operations: 15.9 us -> 1.33 us
  local copies, waits for them, and re-layouts: 33.4 us -> 20.5 us
    pallas_call x0 -> x9, Pallas kernels: none -> 171 us  [exchange(): pl.pallas_call(functools.partial(exchange_kernel, n_dp, n_mp, kinds), out...]
    all_gather x8 -> x0, waiting for transfers between devices: 151 us -> none  [the longest x2 85 us: on_device(): lax.all_gather(mlp_out[layer_index], 'dp', axis=1, tiled=True)]
    all_gather x5 -> x0, blocking collectives: 147 us -> none  [the longest x2 77.4 us: on_device(): lax.all_gather(attn_in[layer_index], 'dp', axis=1, tiled=True)]
    reduce_scatter x4 -> x0, waiting for transfers between devices: 80 us -> none  [reduce_rows(): lax.psum_scatter(partial_value.astype(jnp.bfloat16), 'mp', scatter_dimens...]
    all_to_all x6 -> x0, starting transfers between devices: 24.6 us -> none  [the longest x1 5.51 us: on_device(): lax.all_to_all(send_levels.reshape(peers, heads_dev * READ), 'dp', split_...]
    all_to_all x6 -> x0, waiting for transfers between devices: 21.5 us -> none  [the longest x1 6.54 us: on_device(): lax.all_to_all(send_features.reshape(peers, heads_dev * READ, feature_wid...]
    psum x1 -> x0, blocking collectives: 10.3 us -> none  [on_device(): lax.psum(jnp.einsum('hnd,hdc->hnc', head_features, read_weight, preferred...]
    dot_general x7 -> x13, matrix products: 15.1 us -> 22 us  [the longest x4 12.5 us: dot_turned(): lax.dot_general(left, right, (((1,), (1,)), ((), ())), preferred_element_...]
  transfers between devices with their start and end apart: 18 -> 0, of which waited for: 15 -> 0; matrix products, arithmetic and copies ran while one was open for 6% -> 0% of each run, Pallas kernels for 0% -> 0%
where the time goes in v1:
time: 250 us; the launch traced here: 249 us
  Pallas kernels  171 us (68%)
  matrix products  37.9 us (15%)
  local copies, waits for them, and re-layouts  20.5 us (8%)
  other arithmetic  18.2 us (7%)
    pallas_call x9, Pallas kernels, exchange(): pl.pallas_call(functools.partial(exchange_kernel, n_dp, n_mp, kinds), out...  171 us
    dot_general x4, matrix products, dot_turned(): lax.dot_general(left, right, (((1,), (1,)), ((), ())), preferred_element_...  12.5 us
    dot_general x5, matrix products, dot32(): return jnp.dot(left, right, preferred_element_type=jnp.float32)  6.4 us

profile of v1, /device:TPU:0, one launch (start us, length us, event | category | flops | bytes accessed | tf_op | source)
XLA Modules:
  0.0 249.0 jit_solution(5829200532578751270)
XLA Ops:
  0.7 1.0 select_reduce_fusion
  3.1 1.1 convert_reduce_fusion.2
  4.2 1.2 fusion.28
  7.3 0.8 add_convert_fusion
  8.1 1.6 slice_reduce_fusion
  9.7 0.8 fusion.124
  11.1 0.8 fusion.24.refs_2_
  11.9 0.9 fusion.30.refs_0_
  12.9 0.8 pad_maximum_fusion
  15.2 30.9 %exchange0.1 = (bf16[4,192,768]{2,1,0:T(8,128)(2,1)}, s32[4,3,64]{2,1,0:T(4,128)}, bf16[8,8,128]{2,1,0:T(8,128)(2,1)}, bf16[8,96,768]{2,1,0:T(8,128)(2,1)}) custom-call(bf16[192,768]{1,0:T(8,128)(2,1)} %fusion.30.refs_0_, s32[3,64]{1,0:T(4,128)} %refs_1_.1, bf16[8,8,128]{2,1,0:T(8,128)(2,1)} %fusion.24.refs_2_, bf16[96,768]{1,0:T(8,128)(2,1)} %get-tuple-element.86.refs_3_), custom_call_target="tpu_custom_call" | custom-call | tf_op jit(solution)/shard_map/exchange0/pallas_call | solution.py:186
  46.9 2.5 convolution_convert_fusion.2
  49.4 0.8 fusion.72
  52.6 0.8 copy.74
  53.9 1.3 reshape.355
  55.2 1.3 reshape.354
  56.6 2.9 %fusion.9 = f32[12,3,64,64]{2,3,1,0:T(8,128)} fusion(bf16[12,64,3,64]{1,0,3,2:T(8,128)(2,1)} %reshape.355, bf16[12,64,3,64]{1,0,3,2:T(8,128)(2,1)} %reshape.354, pred[12,64,64]{1,2,0:T(8,128)(4,1)S(1)} %copy-done.7), kind=kOutput, calls=%fused_computation.16 | convolution fusion | flops 19169280 | bytes 1228800 | tf_op jit(solution)/shard_map/sqhd,skhd->shqk/dot_general | solution.py:198
  59.4 2.9 %fusion.10 = bf16[12,64,3,64]{1,3,2,0:T(8,128)(2,1)} fusion(f32[12,3,64,64]{2,3,1,0:T(8,128)} %fusion.9, bf16[12,64,3,64]{1,0,3,2:T(8,128)(2,1)S(1)} %reshape.353), kind=kOutput, calls=%fused_computation.19 | convolution fusion | flops 19319104 | bytes 1179648 | tf_op jit(solution)/shard_map/shqk,skhd->sqhd/dot_general | solution.py:203
  62.4 1.5 copy.72
  64.3 2.7 %convolution_convert_fusion.1 = bf16[768,768]{1,0:T(8,128)(2,1)} fusion(bf16[768,192]{0,1:T(8,128)(2,1)S(1)} %reshape.356, bf16[768,768]{1,0:T(8,128)(2,1)} %bitcast.137), kind=kOutput, calls=%fused_computation.12 | convolution fusion | flops 227082240 | bytes 1867776 | tf_op jit(solution)/shard_map/dot_general | solution.py:212
  67.0 27.8 %exchange1.1 = (bf16[4,192,768]{2,1,0:T(8,128)(2,1)}, bf16[8,96,768]{2,1,0:T(8,128)(2,1)}) custom-call(bf16[4,192,768]{2,1,0:T(8,128)(2,1)} %bitcast.120, bf16[96,768]{1,0:T(8,128)(2,1)} %get-tuple-element.75.refs_1_), custom_call_target="tpu_custom_call" | custom-call | tf_op jit(solution)/shard_map/exchange1/pallas_call | solution.py:186
  94.9 1.5 convert_reduce_fusion.1
  97.0 0.9 multiply_convert_fusion.1.refs_0_
  97.9 26.8 %exchange2.1 = (bf16[4,192,768]{2,1,0:T(8,128)(2,1)}, bf16[8,96,768]{2,1,0:T(8,128)(2,1)}) custom-call(bf16[192,768]{1,0:T(8,128)(2,1)} %multiply_convert_fusion.1.refs_0_, bf16[96,768]{1,0:T(8,128)(2,1)} %get-tuple-element.73.refs_1_), custom_call_target="tpu_custom_call" | custom-call | tf_op jit(solution)/shard_map/exchange2/pallas_call | solution.py:186
  124.7 5.2 %convolution_convert_fusion = bf16[768,768]{1,0:T(8,128)(2,1)} fusion(bf16[768,768]{1,0:T(8,128)(2,1)} %bitcast.147, bf16[768,768]{1,0:T(8,128)(2,1)} %bitcast.146, bf16[768,768]{1,0:T(8,128)(2,1)} %bitcast.144), kind=kOutput, calls=%fused_computation.11 | convolution fusion | flops 1817837568 | bytes 4718592 | tf_op jit(solution)/shard_map/dot_general | solution.py:212
  129.9 26.4 %exchange3.1 = (bf16[4,192,768]{2,1,0:T(8,128)(2,1)}, bf16[8,96,768]{2,1,0:T(8,128)(2,1)}) custom-call(bf16[4,192,768]{2,1,0:T(8,128)(2,1)} %bitcast.123, bf16[96,768]{1,0:T(8,128)(2,1)} %get-tuple-element.87.refs_1_), custom_call_target="tpu_custom_call" | custom-call | tf_op jit(solution)/shard_map/exchange3/pallas_call | solution.py:186
  156.3 1.5 convert_reduce_fusion
  158.9 0.9 multiply_convert_fusion.refs_0_
  159.7 31.4 %exchange4.1 = (bf16[4,192,768]{2,1,0:T(8,128)(2,1)}, f32[4,3,2,768]{3,2,1,0:T(2,128)}, bf16[8,96,768]{2,1,0:T(8,128)(2,1)}, bf16[8,96,768]{2,1,0:T(8,128)(2,1)}) custom-call(bf16[192,768]{1,0:T(8,128)(2,1)} %multiply_convert_fusion.refs_0_, f32[3,2,768]{2,1,0:T(2,128)} %slice.138.refs_1_, bf16[96,768]{1,0:T(8,128)(2,1)} %get-tuple-element.74.refs_2_, ...), custom_call_target="tpu_custom_call" | custom-call | tf_op jit(solution)/shard_map/exchange4/pallas_call | solution.py:186
  191.2 1.0 slice.142
  192.4 2.1 convolution_convert_fusion.3
  195.6 1.4 reshape.365
  196.9 1.7 fusion.23
  198.8 1.9 convolution_convert_fusion.8.refs_0_
  200.7 5.7 %exchange5.1 = bf16[4,24,768]{2,1,0:T(8,128)(2,1)} custom-call(bf16[24,768]{1,0:T(8,128)(2,1)} %convolution_convert_fusion.8.refs_0_), custom_call_target="tpu_custom_call" | custom-call | tf_op jit(solution)/shard_map/exchange5/pallas_call | solution.py:186
  206.4 0.9 convert_reduce_fusion.4
  207.9 2.6 %convolution_convert_fusion.7.refs_0_ = bf16[24,768]{1,0:T(8,128)(2,1)} fusion(bf16[768,768]{1,0:T(8,128)(2,1)} %bitcast.122, bf16[24,768]{1,0:T(8,128)(2,1)S(1)} %convert_element_type.191, bf16[768,768]{1,0:T(8,128)(2,1)S(1)} %bitcast.121), kind=kOutput, calls=%fused_computation.31 | convolution fusion | flops 56807424 | bytes 2433024 | tf_op jit(solution)/shard_map/dot_general | solution.py:212
  210.5 5.7 %exchange6.1 = bf16[4,24,768]{2,1,0:T(8,128)(2,1)} custom-call(bf16[24,768]{1,0:T(8,128)(2,1)} %convolution_convert_fusion.7.refs_0_), custom_call_target="tpu_custom_call" | custom-call | tf_op jit(solution)/shard_map/exchange6/pallas_call | solution.py:186
  216.2 0.9 convert_reduce_fusion.3
  217.7 0.8 fusion.16.refs_0_
  218.6 8.1 %exchange7.1 = bf16[8,8,768]{2,1,0:T(8,128)(2,1)} custom-call(bf16[8,8,768]{2,1,0:T(8,128)(2,1)} %fusion.16.refs_0_), custom_call_target="tpu_custom_call" | custom-call | tf_op jit(solution)/shard_map/exchange7/pallas_call | solution.py:186
  226.7 1.0 reshape.373
  232.9 8.1 %exchange8.1 = bf16[8,8,768]{2,1,0:T(8,128)(2,1)} custom-call(bf16[8,8,768]{2,1,0:T(8,128)(2,1)} %reshape.376.refs_0_), custom_call_target="tpu_custom_call" | custom-call | tf_op jit(solution)/shard_map/exchange8/pallas_call | solution.py:186
  240.9 1.0 convolution_convert_fusion.14
  242.6 1.0 fusion.117
  243.6 0.9 fusion.79
  244.5 1.3 fusion.69
  245.8 1.6 fusion.114
  247.4 1.6 fusion.116
  (138 shorter events, 19.2 us)
Async XLA Ops:
  0.6 227.2 %copy-start = (bf16[4,768,256]{2,1,0:T(8,128)(2,1)S(1)}, bf16[4,768,256]{2,1,0:T(8,128)(2,1)}, u32[]{:S(2)}) copy-start(bf16[4,768,256]{2,1,0:T(8,128)(2,1)} %param.30) | copy-start | bytes 4718596
  0.6 11.3 %copy-start.1 = (bf16[192,768]{1,0:T(8,128)(2,1)S(1)}, bf16[192,768]{1,0:T(8,128)(2,1)}, u32[]{:S(2)}) copy-start(bf16[192,768]{1,0:T(8,128)(2,1)} %param.18) | copy-start | bytes 884740
  0.7 10.4 %copy-start.17 = (bf16[12,2,56]{2,1,0:T(2,128)(2,1)S(1)}, bf16[12,2,56]{2,1,0:T(2,128)(2,1)}, u32[]{:S(2)}) copy-start(bf16[12,2,56]{2,1,0:T(2,128)(2,1)} %param.28) | copy-start | bytes 8068
  0.7 12.2 %copy-start.8 = (bf16[2,3,96,192]{3,2,1,0:T(8,128)(2,1)S(1)}, bf16[2,3,96,192]{3,2,1,0:T(8,128)(2,1)}, u32[]{:S(2)}) copy-start(bf16[2,3,96,192]{3,2,1,0:T(8,128)(2,1)} %param.21) | copy-start | bytes 663556
  10.7 3.0 %copy-start.9 = (bf16[2,96,768]{2,1,0:T(8,128)(2,1)S(1)}, bf16[2,96,768]{2,1,0:T(8,128)(2,1)}, u32[]{:S(2)}) copy-start(bf16[2,96,768]{2,1,0:T(8,128)(2,1)} %param.23) | copy-start | bytes 884740
  11.1 3.3 %copy-start.14 = (bf16[64,24]{0,1:T(8,128)(2,1)}, bf16[64,24]{0,1:T(8,128)(2,1)S(1)}, u32[]{:S(2)}) copy-start(bf16[64,24]{0,1:T(8,128)(2,1)S(1)} %reshape.347) | copy-start | bytes 9220
  11.9 2.5 %copy-start.10 = (bf16[2,768,96]{1,2,0:T(8,128)(2,1)S(1)}, bf16[2,768,96]{1,2,0:T(8,128)(2,1)}, u32[]{:S(2)}) copy-start(bf16[2,768,96]{1,2,0:T(8,128)(2,1)} %param.24) | copy-start | bytes 884740
  49.3 1.6 copy-start.23
  49.3 1.7 copy-start.12
  51.9 0.6 copy-start.6
  53.9 2.7 %copy-start.7 = (pred[12,64,64]{1,2,0:T(8,128)(4,1)S(1)}, pred[12,64,64]{1,2,0:T(8,128)(4,1)}, u32[]{:S(2)}) copy-start(pred[12,64,64]{1,2,0:T(8,128)(4,1)} %copy-done.6) | copy-start | bytes 147460
  96.4 0.7 copy-start.20
  157.8 1.0 copy-start.19
  158.0 34.2 %copy-start.5 = (bf16[8,96,768]{2,1,0:T(8,128)(2,1)S(1)}, bf16[8,96,768]{2,1,0:T(8,128)(2,1)}, u32[]{:S(2)}) copy-start(bf16[8,96,768]{2,1,0:T(8,128)(2,1)} %get-tuple-element.32) | copy-start | bytes 3538948
  194.6 0.7 copy-start.24
  196.9 10.5 %copy-start.13 = (f32[4,3,2,768]{3,2,1,0:T(2,128)S(1)}, f32[4,3,2,768]{3,2,1,0:T(2,128)}, u32[]{:S(2)}) copy-start(f32[4,3,2,768]{3,2,1,0:T(2,128)} %get-tuple-element.30) | copy-start | bytes 221188
  196.9 10.8 %copy-start.22 = (f32[768]{0:T(1024)S(1)}, f32[768]{0:T(1024)}, u32[]{:S(2)}) copy-start(f32[768]{0:T(1024)} %get-tuple-element.60) | copy-start | bytes 9220
  196.9 11.0 %copy-start.4 = (bf16[8,96,768]{2,1,0:T(8,128)(2,1)S(1)}, bf16[8,96,768]{2,1,0:T(8,128)(2,1)}, u32[]{:S(2)}) copy-start(bf16[8,96,768]{2,1,0:T(8,128)(2,1)} %get-tuple-element.33) | copy-start | bytes 3538948
  207.9 9.6 %copy-start.21 = (f32[768]{0:T(1024)S(1)}, f32[768]{0:T(1024)}, u32[]{:S(2)}) copy-start(f32[768]{0:T(1024)} %get-tuple-element.56) | copy-start | bytes 9220
  207.9 9.8 %copy-start.15 = (bf16[64,24]{0,1:T(8,128)(2,1)S(1)}, bf16[64,24]{0,1:T(8,128)(2,1)}, u32[]{:S(2)}) copy-start(bf16[64,24]{0,1:T(8,128)(2,1)} %copy-done.14) | copy-start | bytes 9220
  226.7 1.5 copy-start.11
  226.7 1.5 copy-start.16
  226.7 1.5 copy-start.18
  227.7 1.0 copy-start.2
  227.8 1.1 copy-start.3
  228.2 0.9 copy-start.25
  228.2 0.9 copy-start.26
  228.2 1.0 copy-start.27

commit v2 on v1

--- a/solution.py
+++ b/solution.py
@@ -54,10 +54,21 @@
 
 
 def ring_parts(rows, tile=16):
-    if rows % (2 * tile):
-        return [(0, rows)], []
-    half = rows // 2
-    return [[(way * half + start, tile) for start in range(0, half, tile)] for way in range(2)]
+    if rows % tile:
+        return [(0, rows)]
+    return [(start, tile) for start in range(0, rows, tile)]
+
+
+def ring_step(parts, step, size):
+    count = len(parts)
+    if size % 2 == 0 and step == size // 2 - 1:
+        near = (count + 1) // 2
+        pairs = [(0, chunk) for chunk in range(near)], [(1, chunk) for chunk in range(near, count)]
+        mixed = []
+        for chunk in range(near):
+            mixed += [side[chunk] for side in pairs if chunk < len(side)]
+        return mixed
+    return [(way, chunk) for chunk in range(count) for way in range(2)]
 
 
 def exchange_kernel(n_dp, n_mp, kinds, *refs):
@@ -98,29 +109,27 @@
 
     def ring_copies(item, step):
         source, landing = ins[item], outs[item]
-        made = []
-        for way, parts in enumerate(ring_parts(source.shape[0])):
-            for chunk, (start, extent) in enumerate(parts):
-                origin = ring_index((place + (n_dp - step if way == 0 else step)) % n_dp, n_dp)
-                target = ring_index((place + (1 if way == 0 else n_dp - 1)) % n_dp, n_dp)
-                rows = pl.ds(start, extent)
-                spot = landing.at[origin, rows]
-                made.append(
-                    pltpu.make_async_remote_copy(
-                        src_ref=source.at[rows] if step == 0 else spot,
-                        dst_ref=spot,
-                        send_sem=sems[2 * item].at[step, chunk, way],
-                        recv_sem=sems[2 * item + 1].at[step, chunk, way],
-                        device_id={"dp": target},
-                        device_id_type=MESH_ID,
-                    )
-                )
+        parts = ring_parts(source.shape[0])
+        made = {}
+        for way, chunk in ring_step(parts, step, n_dp):
+            origin = ring_index((place + (n_dp - step if way == 0 else step)) % n_dp, n_dp)
+            target = ring_index((place + (1 if way == 0 else n_dp - 1)) % n_dp, n_dp)
+            rows = pl.ds(*parts[chunk])
+            spot = landing.at[origin, rows]
+            made[way, chunk] = pltpu.make_async_remote_copy(
+                src_ref=source.at[rows] if step == 0 else spot,
+                dst_ref=spot,
+                send_sem=sems[2 * item].at[step, chunk, way],
+                recv_sem=sems[2 * item + 1].at[step, chunk, way],
+                device_id={"dp": target},
+                device_id_type=MESH_ID,
+            )
         return made
 
     rings = [item for item in range(count) if kinds[item] == "ring"]
     flights = {item: ring_copies(item, 0) for item in rings}
     for item in rings:
-        for copy in flights[item]:
+        for copy in flights[item].values():
             copy.start()
     direct = []
     keeps = []
@@ -149,18 +158,21 @@
         )
     for keep in keeps:
         keep.start()
-    sent = [copy for item in rings for copy in flights[item]]
-    for step in range(1, n_dp - 1):
+    sent = [copy for item in rings for copy in flights[item].values()]
+    landed = []
+    for step in range(1, n_dp // 2):
         for item in rings:
             following = ring_copies(item, step)
-            for before, after in zip(flights[item], following):
-                before.wait_recv()
+            for key, after in following.items():
+                flights[item].pop(key).wait_recv()
                 after.start()
+            landed += flights[item].values()
             flights[item] = following
-            sent = sent + following
+            sent += following.values()
     for item in rings:
-        for copy in flights[item]:
-            copy.wait_recv()
+        landed += flights[item].values()
+    for copy in landed:
+        copy.wait_recv()
     for copy in direct:
         copy.wait_recv()
     for copy in sent + direct:
@@ -178,7 +190,7 @@
         lead = {"ring": (n_dp,), "cast": (n_mp,), "split": (), "swap": ()}[kind]
         shapes.append(jax.ShapeDtypeStruct(lead + array.shape, array.dtype))
         if kind == "ring":
-            slots = (n_dp - 1, len(ring_parts(array.shape[0])[0]), 2)
+            slots = (n_dp // 2, len(ring_parts(array.shape[0])), 2)
         else:
             slots = (n_dp if kind == "swap" else n_mp,)
         scratch += [pltpu.SemaphoreType.DMA(slots), pltpu.SemaphoreType.DMA(slots)]

time: 250 us -> 220 us (0.88)
  Pallas kernels: 171 us -> 141 us
    pallas_call x9, Pallas kernels: 171 us -> 141 us  [exchange(): pl.pallas_call(functools.partial(exchange_kernel, n_dp, n_mp, kinds), out...]
where the time goes in v2:
time: 220 us; the launch traced here: 219 us
  Pallas kernels  141 us (64%)
  matrix products  37.9 us (17%)
  local copies, waits for them, and re-layouts  20.5 us (9%)
  other arithmetic  18.2 us (8%)
    pallas_call x9, Pallas kernels, exchange(): pl.pallas_call(functools.partial(exchange_kernel, n_dp, n_mp, kinds), out...  141 us
    dot_general x4, matrix products, dot_turned(): lax.dot_general(left, right, (((1,), (1,)), ((), ())), preferred_element_...  12.5 us
    dot_general x5, matrix products, dot32(): return jnp.dot(left, right, preferred_element_type=jnp.float32)  6.39 us
    reduce_sum x4, other arithmetic, added(): return jnp.sum(blocks.astype(jnp.float32), axis=0)  4.86 us
    dot_general x2, matrix products, attend(): jnp.einsum('shqk,skhd->sqhd', shares, value_rows, preferred_element_type=...  4.65 us

profile of v2, /device:TPU:0, one launch (start us, length us, event | category | flops | bytes accessed | tf_op | source)
XLA Modules:
  0.0 218.8 jit_solution(5256671850950722257)
XLA Ops:
  0.7 1.0 select_reduce_fusion
  3.1 1.1 convert_reduce_fusion.2
  4.2 1.2 fusion.28
  7.3 0.8 add_convert_fusion
  8.1 1.6 slice_reduce_fusion
  9.7 0.8 fusion.124
  11.1 0.8 fusion.24.refs_2_
  11.9 0.9 fusion.30.refs_0_
  12.9 0.8 pad_maximum_fusion
  15.2 24.5 %exchange0.1 = (bf16[4,192,768]{2,1,0:T(8,128)(2,1)}, s32[4,3,64]{2,1,0:T(4,128)}, bf16[8,8,128]{2,1,0:T(8,128)(2,1)}, bf16[8,96,768]{2,1,0:T(8,128)(2,1)}) custom-call(bf16[192,768]{1,0:T(8,128)(2,1)} %fusion.30.refs_0_, s32[3,64]{1,0:T(4,128)} %refs_1_.1, bf16[8,8,128]{2,1,0:T(8,128)(2,1)} %fusion.24.refs_2_, bf16[96,768]{1,0:T(8,128)(2,1)} %get-tuple-element.86.refs_3_), custom_call_target="tpu_custom_call" | custom-call | tf_op jit(solution)/shard_map/exchange0/pallas_call | solution.py:198
  40.4 2.5 %convolution_convert_fusion.2 = bf16[768,576]{0,1:T(8,128)(2,1)S(1)} fusion(bf16[768,768]{1,0:T(8,128)(2,1)} %bitcast.145, bf16[768,768]{1,0:T(8,128)(2,1)} %bitcast.136), kind=kOutput, calls=%fused_computation.13 | convolution fusion | flops 679919616 | bytes 3047424 | tf_op jit(solution)/shard_map/dot_general | solution.py:220
  42.9 0.8 fusion.72
  46.1 0.8 copy.74
  47.4 1.3 reshape.355
  48.7 1.3 reshape.354
  50.1 2.9 %fusion.9 = f32[12,3,64,64]{2,3,1,0:T(8,128)} fusion(bf16[12,64,3,64]{1,0,3,2:T(8,128)(2,1)} %reshape.355, bf16[12,64,3,64]{1,0,3,2:T(8,128)(2,1)} %reshape.354, pred[12,64,64]{1,2,0:T(8,128)(4,1)S(1)} %copy-done.7), kind=kOutput, calls=%fused_computation.16 | convolution fusion | flops 19169280 | bytes 1228800 | tf_op jit(solution)/shard_map/sqhd,skhd->shqk/dot_general | solution.py:210
  53.0 2.9 %fusion.10 = bf16[12,64,3,64]{1,3,2,0:T(8,128)(2,1)} fusion(f32[12,3,64,64]{2,3,1,0:T(8,128)} %fusion.9, bf16[12,64,3,64]{1,0,3,2:T(8,128)(2,1)S(1)} %reshape.353), kind=kOutput, calls=%fused_computation.19 | convolution fusion | flops 19319104 | bytes 1179648 | tf_op jit(solution)/shard_map/shqk,skhd->sqhd/dot_general | solution.py:215
  55.9 1.5 copy.72
  57.8 2.7 %convolution_convert_fusion.1 = bf16[768,768]{1,0:T(8,128)(2,1)} fusion(bf16[768,192]{0,1:T(8,128)(2,1)S(1)} %reshape.356, bf16[768,768]{1,0:T(8,128)(2,1)} %bitcast.137), kind=kOutput, calls=%fused_computation.12 | convolution fusion | flops 227082240 | bytes 1867776 | tf_op jit(solution)/shard_map/dot_general | solution.py:224
  60.5 19.6 %exchange1.1 = (bf16[4,192,768]{2,1,0:T(8,128)(2,1)}, bf16[8,96,768]{2,1,0:T(8,128)(2,1)}) custom-call(bf16[4,192,768]{2,1,0:T(8,128)(2,1)} %bitcast.120, bf16[96,768]{1,0:T(8,128)(2,1)} %get-tuple-element.75.refs_1_), custom_call_target="tpu_custom_call" | custom-call | tf_op jit(solution)/shard_map/exchange1/pallas_call | solution.py:198
  80.1 1.5 convert_reduce_fusion.1
  82.3 0.9 multiply_convert_fusion.1.refs_0_
  83.2 19.3 %exchange2.1 = (bf16[4,192,768]{2,1,0:T(8,128)(2,1)}, bf16[8,96,768]{2,1,0:T(8,128)(2,1)}) custom-call(bf16[192,768]{1,0:T(8,128)(2,1)} %multiply_convert_fusion.1.refs_0_, bf16[96,768]{1,0:T(8,128)(2,1)} %get-tuple-element.73.refs_1_), custom_call_target="tpu_custom_call" | custom-call | tf_op jit(solution)/shard_map/exchange2/pallas_call | solution.py:198
  102.4 5.2 %convolution_convert_fusion = bf16[768,768]{1,0:T(8,128)(2,1)} fusion(bf16[768,768]{1,0:T(8,128)(2,1)} %bitcast.147, bf16[768,768]{1,0:T(8,128)(2,1)} %bitcast.146, bf16[768,768]{1,0:T(8,128)(2,1)} %bitcast.144), kind=kOutput, calls=%fused_computation.11 | convolution fusion | flops 1817837568 | bytes 4718592 | tf_op jit(solution)/shard_map/dot_general | solution.py:224
  107.7 19.8 %exchange3.1 = (bf16[4,192,768]{2,1,0:T(8,128)(2,1)}, bf16[8,96,768]{2,1,0:T(8,128)(2,1)}) custom-call(bf16[4,192,768]{2,1,0:T(8,128)(2,1)} %bitcast.123, bf16[96,768]{1,0:T(8,128)(2,1)} %get-tuple-element.87.refs_1_), custom_call_target="tpu_custom_call" | custom-call | tf_op jit(solution)/shard_map/exchange3/pallas_call | solution.py:198
  127.4 1.5 convert_reduce_fusion
  129.9 0.9 multiply_convert_fusion.refs_0_
  130.8 30.2 %exchange4.1 = (bf16[4,192,768]{2,1,0:T(8,128)(2,1)}, f32[4,3,2,768]{3,2,1,0:T(2,128)}, bf16[8,96,768]{2,1,0:T(8,128)(2,1)}, bf16[8,96,768]{2,1,0:T(8,128)(2,1)}) custom-call(bf16[192,768]{1,0:T(8,128)(2,1)} %multiply_convert_fusion.refs_0_, f32[3,2,768]{2,1,0:T(2,128)} %slice.138.refs_1_, bf16[96,768]{1,0:T(8,128)(2,1)} %get-tuple-element.74.refs_2_, ...), custom_call_target="tpu_custom_call" | custom-call | tf_op jit(solution)/shard_map/exchange4/pallas_call | solution.py:198
  161.0 1.0 slice.142
  162.3 2.1 convolution_convert_fusion.3
  165.4 1.4 reshape.365
  166.7 1.7 fusion.23
  168.6 1.9 convolution_convert_fusion.8.refs_0_
  170.5 5.7 %exchange5.1 = bf16[4,24,768]{2,1,0:T(8,128)(2,1)} custom-call(bf16[24,768]{1,0:T(8,128)(2,1)} %convolution_convert_fusion.8.refs_0_), custom_call_target="tpu_custom_call" | custom-call | tf_op jit(solution)/shard_map/exchange5/pallas_call | solution.py:198
  176.2 0.9 convert_reduce_fusion.4
  177.7 2.6 %convolution_convert_fusion.7.refs_0_ = bf16[24,768]{1,0:T(8,128)(2,1)} fusion(bf16[768,768]{1,0:T(8,128)(2,1)} %bitcast.122, bf16[24,768]{1,0:T(8,128)(2,1)S(1)} %convert_element_type.191, bf16[768,768]{1,0:T(8,128)(2,1)S(1)} %bitcast.121), kind=kOutput, calls=%fused_computation.31 | convolution fusion | flops 56807424 | bytes 2433024 | tf_op jit(solution)/shard_map/dot_general | solution.py:224
  180.3 5.7 %exchange6.1 = bf16[4,24,768]{2,1,0:T(8,128)(2,1)} custom-call(bf16[24,768]{1,0:T(8,128)(2,1)} %convolution_convert_fusion.7.refs_0_), custom_call_target="tpu_custom_call" | custom-call | tf_op jit(solution)/shard_map/exchange6/pallas_call | solution.py:198
  186.0 0.9 convert_reduce_fusion.3
  187.5 0.8 fusion.16.refs_0_
  188.4 8.1 %exchange7.1 = bf16[8,8,768]{2,1,0:T(8,128)(2,1)} custom-call(bf16[8,8,768]{2,1,0:T(8,128)(2,1)} %fusion.16.refs_0_), custom_call_target="tpu_custom_call" | custom-call | tf_op jit(solution)/shard_map/exchange7/pallas_call | solution.py:198
  196.5 1.0 reshape.373
  202.7 8.1 %exchange8.1 = bf16[8,8,768]{2,1,0:T(8,128)(2,1)} custom-call(bf16[8,8,768]{2,1,0:T(8,128)(2,1)} %reshape.376.refs_0_), custom_call_target="tpu_custom_call" | custom-call | tf_op jit(solution)/shard_map/exchange8/pallas_call | solution.py:198
  210.8 1.0 convolution_convert_fusion.14
  212.4 1.0 fusion.117
  213.4 0.9 fusion.79
  214.3 1.3 fusion.69
  215.6 1.6 fusion.114
  217.2 1.6 fusion.116
  (138 shorter events, 19.2 us)
Async XLA Ops:
  0.6 197.0 %copy-start = (bf16[4,768,256]{2,1,0:T(8,128)(2,1)S(1)}, bf16[4,768,256]{2,1,0:T(8,128)(2,1)}, u32[]{:S(2)}) copy-start(bf16[4,768,256]{2,1,0:T(8,128)(2,1)} %param.30) | copy-start | bytes 4718596
  0.6 11.3 %copy-start.1 = (bf16[192,768]{1,0:T(8,128)(2,1)S(1)}, bf16[192,768]{1,0:T(8,128)(2,1)}, u32[]{:S(2)}) copy-start(bf16[192,768]{1,0:T(8,128)(2,1)} %param.18) | copy-start | bytes 884740
  0.7 10.4 %copy-start.17 = (bf16[12,2,56]{2,1,0:T(2,128)(2,1)S(1)}, bf16[12,2,56]{2,1,0:T(2,128)(2,1)}, u32[]{:S(2)}) copy-start(bf16[12,2,56]{2,1,0:T(2,128)(2,1)} %param.28) | copy-start | bytes 8068
  0.7 12.2 %copy-start.8 = (bf16[2,3,96,192]{3,2,1,0:T(8,128)(2,1)S(1)}, bf16[2,3,96,192]{3,2,1,0:T(8,128)(2,1)}, u32[]{:S(2)}) copy-start(bf16[2,3,96,192]{3,2,1,0:T(8,128)(2,1)} %param.21) | copy-start | bytes 663556
  10.7 3.0 %copy-start.9 = (bf16[2,96,768]{2,1,0:T(8,128)(2,1)S(1)}, bf16[2,96,768]{2,1,0:T(8,128)(2,1)}, u32[]{:S(2)}) copy-start(bf16[2,96,768]{2,1,0:T(8,128)(2,1)} %param.23) | copy-start | bytes 884740
  11.1 3.3 %copy-start.14 = (bf16[64,24]{0,1:T(8,128)(2,1)}, bf16[64,24]{0,1:T(8,128)(2,1)S(1)}, u32[]{:S(2)}) copy-start(bf16[64,24]{0,1:T(8,128)(2,1)S(1)} %reshape.347) | copy-start | bytes 9220
  11.9 2.5 %copy-start.10 = (bf16[2,768,96]{1,2,0:T(8,128)(2,1)S(1)}, bf16[2,768,96]{1,2,0:T(8,128)(2,1)}, u32[]{:S(2)}) copy-start(bf16[2,768,96]{1,2,0:T(8,128)(2,1)} %param.24) | copy-start | bytes 884740
  42.8 1.6 copy-start.23
  42.8 1.7 copy-start.12
  45.5 0.6 copy-start.6
  47.4 2.7 %copy-start.7 = (pred[12,64,64]{1,2,0:T(8,128)(4,1)S(1)}, pred[12,64,64]{1,2,0:T(8,128)(4,1)}, u32[]{:S(2)}) copy-start(pred[12,64,64]{1,2,0:T(8,128)(4,1)} %copy-done.6) | copy-start | bytes 147460
  81.6 0.7 copy-start.20
  128.9 1.0 copy-start.19
  129.1 32.9 %copy-start.5 = (bf16[8,96,768]{2,1,0:T(8,128)(2,1)S(1)}, bf16[8,96,768]{2,1,0:T(8,128)(2,1)}, u32[]{:S(2)}) copy-start(bf16[8,96,768]{2,1,0:T(8,128)(2,1)} %get-tuple-element.32) | copy-start | bytes 3538948
  164.4 0.7 copy-start.24
  166.7 10.5 %copy-start.13 = (f32[4,3,2,768]{3,2,1,0:T(2,128)S(1)}, f32[4,3,2,768]{3,2,1,0:T(2,128)}, u32[]{:S(2)}) copy-start(f32[4,3,2,768]{3,2,1,0:T(2,128)} %get-tuple-element.30) | copy-start | bytes 221188
  166.7 10.8 %copy-start.22 = (f32[768]{0:T(1024)S(1)}, f32[768]{0:T(1024)}, u32[]{:S(2)}) copy-start(f32[768]{0:T(1024)} %get-tuple-element.60) | copy-start | bytes 9220
  166.7 11.0 %copy-start.4 = (bf16[8,96,768]{2,1,0:T(8,128)(2,1)S(1)}, bf16[8,96,768]{2,1,0:T(8,128)(2,1)}, u32[]{:S(2)}) copy-start(bf16[8,96,768]{2,1,0:T(8,128)(2,1)} %get-tuple-element.33) | copy-start | bytes 3538948
  177.7 9.6 %copy-start.21 = (f32[768]{0:T(1024)S(1)}, f32[768]{0:T(1024)}, u32[]{:S(2)}) copy-start(f32[768]{0:T(1024)} %get-tuple-element.56) | copy-start | bytes 9220
  177.7 9.8 %copy-start.15 = (bf16[64,24]{0,1:T(8,128)(2,1)S(1)}, bf16[64,24]{0,1:T(8,128)(2,1)}, u32[]{:S(2)}) copy-start(bf16[64,24]{0,1:T(8,128)(2,1)} %copy-done.14) | copy-start | bytes 9220
  196.5 1.5 copy-start.11
  196.5 1.5 copy-start.16
  196.5 1.5 copy-start.18
  197.5 1.0 copy-start.2
  197.7 1.1 copy-start.3
  198.0 0.9 copy-start.25
  198.0 0.9 copy-start.26
  198.0 1.0 copy-start.27
